TPU v7x, 32 devices: a whole 2x2x4 slice. The times are simulated.
32 devices in a mesh: gx: 4 (over z), gy: 4 (over x, core), gz: 2 (over y).
Axes of the slice: x: 2, y: 2, z: 4, core: 2. Of those that a mesh axis runs over, the one named last changes fastest.
Arguments:
- residual: float32 [32, 32, 256], P('gx', 'gy', 'gz'), may hold values from -18 to 18
- direction: float32 [32, 32, 256], P('gx', 'gy', 'gz'), may hold values from -18 to 18
Outputs:
- powers: float32 [2, 4, 32, 32, 256], P(None, None, 'gx', 'gy', 'gz')
- gram_matrix: float32 [9, 9], replicated
- projections: float32 [9], replicated
All inputs are finite; a program needn't handle non-finite values.
Results may differ from a plain program's by a relative error of at most 0.00029.
Values sent between devices are 32-bit elements; how exact they have to be, the bound alone decides.
A program may use at most 64 MiB of HBM per device.

v0:
```python
import jax
import jax.numpy as jnp
from jax import lax
from jax.sharding import PartitionSpec as P

STEPS = 4
MARGIN = 1
SWEEPS = 3


SWEEP_SCALE = 1.0 / 9.0


def extended(cells, sides, width):
    for axis, dim in sides:
        count = lax.axis_size(axis)
        ends = count - 1
        head = lax.slice_in_dim(cells, 0, width, axis=dim)
        tail = lax.slice_in_dim(cells, cells.shape[dim] - width, cells.shape[dim], axis=dim)
        cells = jnp.concatenate(
            [
                lax.ppermute(tail, axis, [(i, (i + 1) % count) for i in range(ends)]),
                cells,
                lax.ppermute(head, axis, [((i + 1) % count, i) for i in range(ends)]),
            ],
            axis=dim,
        )
    return cells


def stencil_image(padded):
    center = padded[:, 1:-1, 1:-1, 1:-1]
    beside = padded[:, 2:, 1:-1, 1:-1] + padded[:, :-2, 1:-1, 1:-1]
    beside = beside + padded[:, 1:-1, 2:, 1:-1] + padded[:, 1:-1, :-2, 1:-1]
    beside = beside + padded[:, 1:-1, 1:-1, 2:] + padded[:, 1:-1, 1:-1, :-2]
    return 6.0 * center - beside


def pad_along(values, dimension, before, after):
    widths = [(0, 0)] * values.ndim
    widths[dimension] = (before, after)
    return jnp.pad(values, widths)


def assemble(received, reach, growth):
    for dimension in (1, 2, 3):
        length = received.shape[dimension] - 2 * reach
        result_len = length + 2 * growth
        middle = lax.slice_in_dim(received, reach, reach + length, axis=dimension)
        middle = pad_along(middle, dimension, growth, growth)
        below_part = lax.slice_in_dim(received, 0, reach, axis=dimension)
        above_part = lax.slice_in_dim(received, reach + length, 2 * reach + length, axis=dimension)
        received = (
            middle
            + pad_along(below_part, dimension, 0, result_len - reach)
            + pad_along(above_part, dimension, result_len - reach, 0)
        )
    return received


def inside_profile(position, cells, devices, margin):
    global_spots = position * cells - margin + jnp.arange(cells + 2 * margin, dtype=jnp.int32)
    return jnp.logical_and(global_spots >= 0, global_spots < devices * cells).astype(jnp.float32)


def grid_mask(cells_x, cells_y, cells_z, margin):
    along_x = inside_profile(lax.axis_index("gx"), cells_x, lax.axis_size("gx"), margin)
    along_y = inside_profile(lax.axis_index("gy"), cells_y, lax.axis_size("gy"), margin)
    along_z = inside_profile(lax.axis_index("gz"), cells_z, lax.axis_size("gz"), margin)
    return along_x[:, None, None] * along_y[None, :, None] * along_z[None, None, :]


def subdomain_solve(source, mask):
    source = mask * source
    iterate = mask * (SWEEP_SCALE * source)
    for sweep_index in range(SWEEPS - 1):
        padded = jnp.pad(iterate, ((0, 0), (1, 1), (1, 1), (1, 1)))
        iterate = mask * (iterate + SWEEP_SCALE * (source - stencil_image(padded)))
    return iterate


def flatten_rows(fields):
    return jnp.stack([member_field.reshape(-1) for member_field in fields])


def inner_table(left_rows, right_rows):
    return jnp.einsum("ac,bc->ab", left_rows, right_rows, precision=lax.Precision.HIGHEST)


def inner_vector(left_rows, target):
    return jnp.einsum("ac,c->a", left_rows, target, precision=lax.Precision.HIGHEST)


def local(residual, direction):
    margin = MARGIN
    cells_x, cells_y, cells_z = residual.shape
    mask = grid_mask(cells_x, cells_y, cells_z, margin)
    cell_count = float(
        lax.axis_size("gx")
        * cells_x
        * lax.axis_size("gy")
        * cells_y
        * lax.axis_size("gz")
        * cells_z
    )
    target = residual.reshape(-1)
    pieces = jnp.pad(
        jnp.stack([direction, residual]),
        ((0, 0), (margin, margin), (margin, margin), (margin, margin)),
    )
    p_fields, p_images, z_fields, z_images = ([], [], [], [])
    for step_index in range(STEPS + 1):
        final_step = step_index == STEPS
        source = None
        deep_reach = 2 * margin + 1
        received = extended(pieces, (("gx", 1), ("gy", 2), ("gz", 3)), deep_reach)
        region = assemble(received, deep_reach, 1)
        fields = region[
            :,
            margin + 1 : margin + 1 + cells_x,
            margin + 1 : margin + 1 + cells_y,
            margin + 1 : margin + 1 + cells_z,
        ]
        if final_step:
            own_images = stencil_image(
                region[
                    :,
                    margin : margin + cells_x + 2,
                    margin : margin + cells_y + 2,
                    margin : margin + cells_z + 2,
                ]
            )
        else:
            wide_images = stencil_image(region)
            own_images = wide_images[
                :, margin : margin + cells_x, margin : margin + cells_y, margin : margin + cells_z
            ]
            if step_index == 0:
                source = jnp.stack([wide_images[0], region[1, 1:-1, 1:-1, 1:-1]])
            else:
                source = wide_images
        p_fields.append(fields[0])
        p_images.append(own_images[0])
        if step_index > 0:
            z_fields.append(fields[1])
            z_images.append(own_images[1])
        if not final_step:
            pieces = subdomain_solve(source, mask)
    basis_rows = flatten_rows(p_fields + z_fields)
    image_rows = flatten_rows(p_images + z_images)
    gram_sum, projection_sum = lax.psum(
        (inner_table(basis_rows, image_rows), inner_vector(basis_rows, target)), ("gx", "gy", "gz")
    )
    powers = jnp.stack([jnp.stack(p_fields[1:]), jnp.stack(z_fields)])
    return (powers, gram_sum / cell_count, projection_sum / cell_count)


def solution(mesh):
    placed = (P("gx", "gy", "gz"), P("gx", "gy", "gz"))
    return jax.shard_map(
        local,
        mesh=mesh,
        in_specs=placed,
        out_specs=(P(None, None, "gx", "gy", "gz"), P(), P()),
        check_vma=False,
    )
```

profile of v0, /device:TPU:0, one launch (start us, length us, event | category | flops | bytes accessed | tf_op | source)
XLA Modules:
  0.0 197.6 jit_solution(4123972771521606894)
XLA Ops:
  1.6 5.0 %collective-permute-start = (f32[2,3,10,130]{3,2,1,0:T(8,128)S(1)}, f32[2,3,10,130]{3,2,1,0:T(8,128)S(1)}, u32[]{:S(2)}, u32[]{:S(2)}) collective-permute-start(f32[2,3,10,130]{3,2,1,0:T(8,128)S(1)} %get-tuple-element.53), channel_id=1, source_target_pairs={{0,8},{8,16},{16,24},{1,9},{9,17},{17,25},{2,10},{10,18},{18,26},{... | collective-permute-start | bytes 93608 | tf_op jit(solution)/shard_map/ppermute | solution.py:22
  8.7 4.3 %collective-permute-done.1 = f32[2,3,10,130]{3,2,1,0:T(8,128)S(1)} collective-permute-done((f32[2,3,10,130]{3,2,1,0:T(8,128)S(1)}, f32[2,3,10,130]{3,2,1,0:T(8,128)S(1)}, u32[]{:S(2)}, u32[]{:S(2)}) %collective-permute-start.1) | collective-permute-done | bytes 31232 | tf_op jit(solution)/shard_map/ppermute | solution.py:24
  15.7 3.6 %collective-permute-done.3 = f32[2,16,3,130]{3,2,1,0:T(4,128)S(1)} collective-permute-done((f32[2,16,3,130]{3,2,1,0:T(4,128)S(1)}, f32[2,16,3,130]{3,2,1,0:T(4,128)S(1)}, u32[]{:S(2)}, u32[]{:S(2)}) %collective-permute-start.3) | collective-permute-done | bytes 49952 | tf_op jit(solution)/shard_map/ppermute | solution.py:24
  19.6 3.4 %collective-permute-start.4 = (f32[2,16,16,3]{3,2,1,0:T(8,128)S(1)}, f32[2,16,16,3]{3,2,1,0:T(8,128)S(1)}, u32[]{:S(2)}, u32[]{:S(2)}) collective-permute-start(f32[2,16,16,3]{3,2,1,0:T(8,128)S(1)} %get-tuple-element.27), channel_id=1, source_target_pairs={{0,1},{2,3},{4,5},{6,7},{8,9},{10,11},{12,13},{14,15},{16,17},{18,... | collective-permute-start | bytes 18440 | tf_op jit(solution)/shard_map/ppermute | solution.py:22
  24.5 2.7 %collective-permute-done.4 = f32[2,16,16,3]{3,2,1,0:T(8,128)S(1)} collective-permute-done((f32[2,16,16,3]{3,2,1,0:T(8,128)S(1)}, f32[2,16,16,3]{3,2,1,0:T(8,128)S(1)}, u32[]{:S(2)}, u32[]{:S(2)}) %collective-permute-start.4) | collective-permute-done | bytes 6176 | tf_op jit(solution)/shard_map/ppermute | solution.py:22
  27.2 4.7 %collective-permute-done.5 = f32[2,16,16,3]{3,2,1,0:T(8,128)S(1)} collective-permute-done((f32[2,16,16,3]{3,2,1,0:T(8,128)S(1)}, f32[2,16,16,3]{3,2,1,0:T(8,128)S(1)}, u32[]{:S(2)}, u32[]{:S(2)}) %collective-permute-start.5) | collective-permute-done | bytes 6176 | tf_op jit(solution)/shard_map/ppermute | solution.py:24
  35.8 3.5 %collective-permute-start.6 = (f32[2,3,10,130]{3,2,1,0:T(8,128)S(1)}, f32[2,3,10,130]{3,2,1,0:T(8,128)S(1)}, u32[]{:S(2)}, u32[]{:S(2)}) collective-permute-start(f32[2,3,10,130]{3,2,1,0:T(8,128)S(1)} %get-tuple-element.51), channel_id=1, source_target_pairs={{0,8},{8,16},{16,24},{1,9},{9,17},{17,25},{2,10},{10,18},{18,26},{... | collective-permute-start | bytes 93608 | tf_op jit(solution)/shard_map/ppermute | solution.py:22
  41.5 4.5 %collective-permute-done.7 = f32[2,3,10,130]{3,2,1,0:T(8,128)S(1)} collective-permute-done((f32[2,3,10,130]{3,2,1,0:T(8,128)S(1)}, f32[2,3,10,130]{3,2,1,0:T(8,128)S(1)}, u32[]{:S(2)}, u32[]{:S(2)}) %collective-permute-start.7) | collective-permute-done | bytes 31232 | tf_op jit(solution)/shard_map/ppermute | solution.py:24
  49.9 3.5 %collective-permute-done.9 = f32[2,16,3,130]{3,2,1,0:T(4,128)S(1)} collective-permute-done((f32[2,16,3,130]{3,2,1,0:T(4,128)S(1)}, f32[2,16,3,130]{3,2,1,0:T(4,128)S(1)}, u32[]{:S(2)}, u32[]{:S(2)}) %collective-permute-start.9) | collective-permute-done | bytes 49952 | tf_op jit(solution)/shard_map/ppermute | solution.py:24
  59.1 4.7 %collective-permute-done.11 = f32[2,16,16,3]{3,2,1,0:T(8,128)S(1)} collective-permute-done((f32[2,16,16,3]{3,2,1,0:T(8,128)S(1)}, f32[2,16,16,3]{3,2,1,0:T(8,128)S(1)}, u32[]{:S(2)}, u32[]{:S(2)}) %collective-permute-start.11) | collective-permute-done | bytes 6176 | tf_op jit(solution)/shard_map/ppermute | solution.py:24
  66.4 3.5 %collective-permute-start.12 = (f32[2,3,10,130]{3,2,1,0:T(8,128)S(1)}, f32[2,3,10,130]{3,2,1,0:T(8,128)S(1)}, u32[]{:S(2)}, u32[]{:S(2)}) collective-permute-start(f32[2,3,10,130]{3,2,1,0:T(8,128)S(1)} %get-tuple-element.49), channel_id=1, source_target_pairs={{0,8},{8,16},{16,24},{1,9},{9,17},{17,25},{2,10},{10,18},{18,26},{... | collective-permute-start | bytes 93608 | tf_op jit(solution)/shard_map/ppermute | solution.py:22
  72.1 4.4 %collective-permute-done.13 = f32[2,3,10,130]{3,2,1,0:T(8,128)S(1)} collective-permute-done((f32[2,3,10,130]{3,2,1,0:T(8,128)S(1)}, f32[2,3,10,130]{3,2,1,0:T(8,128)S(1)}, u32[]{:S(2)}, u32[]{:S(2)}) %collective-permute-start.13) | collective-permute-done | bytes 31232 | tf_op jit(solution)/shard_map/ppermute | solution.py:24
  76.5 2.7 %collective-permute-start.14 = (f32[2,16,3,130]{3,2,1,0:T(4,128)S(1)}, f32[2,16,3,130]{3,2,1,0:T(4,128)S(1)}, u32[]{:S(2)}, u32[]{:S(2)}) collective-permute-start(f32[2,16,3,130]{3,2,1,0:T(4,128)S(1)} %get-tuple-element.21), channel_id=1, source_target_pairs={{0,2},{2,4},{4,6},{1,3},{3,5},{5,7},{8,10},{10,12},{12,14},{9,11},... | collective-permute-start | bytes 149768 | tf_op jit(solution)/shard_map/ppermute | solution.py:22
  80.5 3.6 %collective-permute-done.15 = f32[2,16,3,130]{3,2,1,0:T(4,128)S(1)} collective-permute-done((f32[2,16,3,130]{3,2,1,0:T(4,128)S(1)}, f32[2,16,3,130]{3,2,1,0:T(4,128)S(1)}, u32[]{:S(2)}, u32[]{:S(2)}) %collective-permute-start.15) | collective-permute-done | bytes 49952 | tf_op jit(solution)/shard_map/ppermute | solution.py:24
  89.8 4.7 %collective-permute-done.17 = f32[2,16,16,3]{3,2,1,0:T(8,128)S(1)} collective-permute-done((f32[2,16,16,3]{3,2,1,0:T(8,128)S(1)}, f32[2,16,16,3]{3,2,1,0:T(8,128)S(1)}, u32[]{:S(2)}, u32[]{:S(2)}) %collective-permute-start.17) | collective-permute-done | bytes 6176 | tf_op jit(solution)/shard_map/ppermute | solution.py:24
  101.2 4.4 %collective-permute-done.19 = f32[2,3,10,130]{3,2,1,0:T(8,128)S(1)} collective-permute-done((f32[2,3,10,130]{3,2,1,0:T(8,128)S(1)}, f32[2,3,10,130]{3,2,1,0:T(8,128)S(1)}, u32[]{:S(2)}, u32[]{:S(2)}) %collective-permute-start.19) | collective-permute-done | bytes 31232 | tf_op jit(solution)/shard_map/ppermute | solution.py:24
  105.7 2.7 %collective-permute-start.20 = (f32[2,16,3,130]{3,2,1,0:T(4,128)S(1)}, f32[2,16,3,130]{3,2,1,0:T(4,128)S(1)}, u32[]{:S(2)}, u32[]{:S(2)}) collective-permute-start(f32[2,16,3,130]{3,2,1,0:T(4,128)S(1)} %get-tuple-element.17), channel_id=1, source_target_pairs={{0,2},{2,4},{4,6},{1,3},{3,5},{5,7},{8,10},{10,12},{12,14},{9,11},... | collective-permute-start | bytes 149768 | tf_op jit(solution)/shard_map/ppermute | solution.py:22
  109.8 3.5 %collective-permute-done.21 = f32[2,16,3,130]{3,2,1,0:T(4,128)S(1)} collective-permute-done((f32[2,16,3,130]{3,2,1,0:T(4,128)S(1)}, f32[2,16,3,130]{3,2,1,0:T(4,128)S(1)}, u32[]{:S(2)}, u32[]{:S(2)}) %collective-permute-start.21) | collective-permute-done | bytes 49952 | tf_op jit(solution)/shard_map/ppermute | solution.py:24
  119.0 4.7 %collective-permute-done.23 = f32[2,16,16,3]{3,2,1,0:T(8,128)S(1)} collective-permute-done((f32[2,16,16,3]{3,2,1,0:T(8,128)S(1)}, f32[2,16,16,3]{3,2,1,0:T(8,128)S(1)}, u32[]{:S(2)}, u32[]{:S(2)}) %collective-permute-start.23) | collective-permute-done | bytes 6176 | tf_op jit(solution)/shard_map/ppermute | solution.py:24
  130.4 4.4 %collective-permute-done.25 = f32[2,3,10,130]{3,2,1,0:T(8,128)S(1)} collective-permute-done((f32[2,3,10,130]{3,2,1,0:T(8,128)S(1)}, f32[2,3,10,130]{3,2,1,0:T(8,128)S(1)}, u32[]{:S(2)}, u32[]{:S(2)}) %collective-permute-start.25) | collective-permute-done | bytes 31232 | tf_op jit(solution)/shard_map/ppermute | solution.py:24
  134.8 2.7 %collective-permute-start.26 = (f32[2,16,3,130]{3,2,1,0:T(4,128)S(1)}, f32[2,16,3,130]{3,2,1,0:T(4,128)S(1)}, u32[]{:S(2)}, u32[]{:S(2)}) collective-permute-start(f32[2,16,3,130]{3,2,1,0:T(4,128)S(1)} %get-tuple-element.13), channel_id=1, source_target_pairs={{0,2},{2,4},{4,6},{1,3},{3,5},{5,7},{8,10},{10,12},{12,14},{9,11},... | collective-permute-start | bytes 149768 | tf_op jit(solution)/shard_map/ppermute | solution.py:22
  139.0 3.5 %collective-permute-done.27 = f32[2,16,3,130]{3,2,1,0:T(4,128)S(1)} collective-permute-done((f32[2,16,3,130]{3,2,1,0:T(4,128)S(1)}, f32[2,16,3,130]{3,2,1,0:T(4,128)S(1)}, u32[]{:S(2)}, u32[]{:S(2)}) %collective-permute-start.27) | collective-permute-done | bytes 49952 | tf_op jit(solution)/shard_map/ppermute | solution.py:24
  148.2 4.7 %collective-permute-done.29 = f32[2,16,16,3]{3,2,1,0:T(8,128)S(1)} collective-permute-done((f32[2,16,16,3]{3,2,1,0:T(8,128)S(1)}, f32[2,16,16,3]{3,2,1,0:T(8,128)S(1)}, u32[]{:S(2)}, u32[]{:S(2)}) %collective-permute-start.29) | collective-permute-done | bytes 6176 | tf_op jit(solution)/shard_map/ppermute | solution.py:24
  156.9 38.8 %all-reduce.39 = (f32[9,9]{1,0:T(8,128)S(1)}, f32[9]{0:T(128)S(1)}) all-reduce(f32[9,9]{1,0:T(8,128)S(1)} %fusion.151, f32[9]{0:T(128)S(1)} %convolution_bitcast_fusion), channel_id=1, replica_groups=mesh['gx'=4,'gy'=4,'gz'=2] {'gx','gy','gz'}, use_global_device_ids=true, to_apply=%region_0.1 | all-reduce | flops 90 | bytes 720 | tf_op jit(solution)/shard_map/psum | solution.py:151
  (148 shorter events, 68.0 us)
Async XLA Ops:
  1.6 7.2 %collective-permute-start = (f32[2,3,10,130]{3,2,1,0:T(8,128)S(1)}, f32[2,3,10,130]{3,2,1,0:T(8,128)S(1)}, u32[]{:S(2)}, u32[]{:S(2)}) collective-permute-start(f32[2,3,10,130]{3,2,1,0:T(8,128)S(1)} %get-tuple-element.53), channel_id=1, source_target_pairs={{0,8},{8,16},{16,24},{1,9},{9,17},{17,25},{2,10},{10,18},{18,26},{... | collective-permute-start | bytes 93608 | tf_op jit(solution)/shard_map/ppermute | solution.py:22
  6.5 6.5 %collective-permute-start.1 = (f32[2,3,10,130]{3,2,1,0:T(8,128)S(1)}, f32[2,3,10,130]{3,2,1,0:T(8,128)S(1)}, u32[]{:S(2)}, u32[]{:S(2)}) collective-permute-start(f32[2,3,10,130]{3,2,1,0:T(8,128)S(1)} %get-tuple-element.54), channel_id=1, source_target_pairs={{8,0},{16,8},{24,16},{9,1},{17,9},{25,17},{10,2},{18,10},{26,18},{... | collective-permute-start | bytes 93608 | tf_op jit(solution)/shard_map/ppermute | solution.py:24
  14.4 5.0 %collective-permute-start.3 = (f32[2,16,3,130]{3,2,1,0:T(4,128)S(1)}, f32[2,16,3,130]{3,2,1,0:T(4,128)S(1)}, u32[]{:S(2)}, u32[]{:S(2)}) collective-permute-start(f32[2,16,3,130]{3,2,1,0:T(4,128)S(1)} %get-tuple-element.30), channel_id=1, source_target_pairs={{2,0},{4,2},{6,4},{3,1},{5,3},{7,5},{10,8},{12,10},{14,12},{11,9},... | collective-permute-start | bytes 149768 | tf_op jit(solution)/shard_map/ppermute | solution.py:24
  19.6 7.5 %collective-permute-start.4 = (f32[2,16,16,3]{3,2,1,0:T(8,128)S(1)}, f32[2,16,16,3]{3,2,1,0:T(8,128)S(1)}, u32[]{:S(2)}, u32[]{:S(2)}) collective-permute-start(f32[2,16,16,3]{3,2,1,0:T(8,128)S(1)} %get-tuple-element.27), channel_id=1, source_target_pairs={{0,1},{2,3},{4,5},{6,7},{8,9},{10,11},{12,13},{14,15},{16,17},{18,... | collective-permute-start | bytes 18440 | tf_op jit(solution)/shard_map/ppermute | solution.py:22
  23.1 8.8 %collective-permute-start.5 = (f32[2,16,16,3]{3,2,1,0:T(8,128)S(1)}, f32[2,16,16,3]{3,2,1,0:T(8,128)S(1)}, u32[]{:S(2)}, u32[]{:S(2)}) collective-permute-start(f32[2,16,16,3]{3,2,1,0:T(8,128)S(1)} %get-tuple-element.28), channel_id=1, source_target_pairs={{1,0},{3,2},{5,4},{7,6},{9,8},{11,10},{13,12},{15,14},{17,16},{19,... | collective-permute-start | bytes 18440 | tf_op jit(solution)/shard_map/ppermute | solution.py:24
  35.8 5.7 %collective-permute-start.6 = (f32[2,3,10,130]{3,2,1,0:T(8,128)S(1)}, f32[2,3,10,130]{3,2,1,0:T(8,128)S(1)}, u32[]{:S(2)}, u32[]{:S(2)}) collective-permute-start(f32[2,3,10,130]{3,2,1,0:T(8,128)S(1)} %get-tuple-element.51), channel_id=1, source_target_pairs={{0,8},{8,16},{16,24},{1,9},{9,17},{17,25},{2,10},{10,18},{18,26},{... | collective-permute-start | bytes 93608 | tf_op jit(solution)/shard_map/ppermute | solution.py:22
  39.3 6.7 %collective-permute-start.7 = (f32[2,3,10,130]{3,2,1,0:T(8,128)S(1)}, f32[2,3,10,130]{3,2,1,0:T(8,128)S(1)}, u32[]{:S(2)}, u32[]{:S(2)}) collective-permute-start(f32[2,3,10,130]{3,2,1,0:T(8,128)S(1)} %get-tuple-element.52), channel_id=1, source_target_pairs={{8,0},{16,8},{24,16},{9,1},{17,9},{25,17},{10,2},{18,10},{26,18},{... | collective-permute-start | bytes 93608 | tf_op jit(solution)/shard_map/ppermute | solution.py:24
  48.6 4.8 %collective-permute-start.9 = (f32[2,16,3,130]{3,2,1,0:T(4,128)S(1)}, f32[2,16,3,130]{3,2,1,0:T(4,128)S(1)}, u32[]{:S(2)}, u32[]{:S(2)}) collective-permute-start(f32[2,16,3,130]{3,2,1,0:T(4,128)S(1)} %get-tuple-element.26), channel_id=1, source_target_pairs={{2,0},{4,2},{6,4},{3,1},{5,3},{7,5},{10,8},{12,10},{14,12},{11,9},... | collective-permute-start | bytes 149768 | tf_op jit(solution)/shard_map/ppermute | solution.py:24
  53.7 5.4 %collective-permute-start.10 = (f32[2,16,16,3]{3,2,1,0:T(8,128)S(1)}, f32[2,16,16,3]{3,2,1,0:T(8,128)S(1)}, u32[]{:S(2)}, u32[]{:S(2)}) collective-permute-start(f32[2,16,16,3]{3,2,1,0:T(8,128)S(1)} %get-tuple-element.23), channel_id=1, source_target_pairs={{0,1},{2,3},{4,5},{6,7},{8,9},{10,11},{12,13},{14,15},{16,17},{18,... | collective-permute-start | bytes 18440 | tf_op jit(solution)/shard_map/ppermute | solution.py:22
  55.1 8.7 %collective-permute-start.11 = (f32[2,16,16,3]{3,2,1,0:T(8,128)S(1)}, f32[2,16,16,3]{3,2,1,0:T(8,128)S(1)}, u32[]{:S(2)}, u32[]{:S(2)}) collective-permute-start(f32[2,16,16,3]{3,2,1,0:T(8,128)S(1)} %get-tuple-element.24), channel_id=1, source_target_pairs={{1,0},{3,2},{5,4},{7,6},{9,8},{11,10},{13,12},{15,14},{17,16},{19,... | collective-permute-start | bytes 18440 | tf_op jit(solution)/shard_map/ppermute | solution.py:24
  66.4 5.7 %collective-permute-start.12 = (f32[2,3,10,130]{3,2,1,0:T(8,128)S(1)}, f32[2,3,10,130]{3,2,1,0:T(8,128)S(1)}, u32[]{:S(2)}, u32[]{:S(2)}) collective-permute-start(f32[2,3,10,130]{3,2,1,0:T(8,128)S(1)} %get-tuple-element.49), channel_id=1, source_target_pairs={{0,8},{8,16},{16,24},{1,9},{9,17},{17,25},{2,10},{10,18},{18,26},{... | collective-permute-start | bytes 93608 | tf_op jit(solution)/shard_map/ppermute | solution.py:22
  69.9 6.6 %collective-permute-start.13 = (f32[2,3,10,130]{3,2,1,0:T(8,128)S(1)}, f32[2,3,10,130]{3,2,1,0:T(8,128)S(1)}, u32[]{:S(2)}, u32[]{:S(2)}) collective-permute-start(f32[2,3,10,130]{3,2,1,0:T(8,128)S(1)} %get-tuple-element.50), channel_id=1, source_target_pairs={{8,0},{16,8},{24,16},{9,1},{17,9},{25,17},{10,2},{18,10},{26,18},{... | collective-permute-start | bytes 93608 | tf_op jit(solution)/shard_map/ppermute | solution.py:24
  79.2 4.9 %collective-permute-start.15 = (f32[2,16,3,130]{3,2,1,0:T(4,128)S(1)}, f32[2,16,3,130]{3,2,1,0:T(4,128)S(1)}, u32[]{:S(2)}, u32[]{:S(2)}) collective-permute-start(f32[2,16,3,130]{3,2,1,0:T(4,128)S(1)} %get-tuple-element.22), channel_id=1, source_target_pairs={{2,0},{4,2},{6,4},{3,1},{5,3},{7,5},{10,8},{12,10},{14,12},{11,9},... | collective-permute-start | bytes 149768 | tf_op jit(solution)/shard_map/ppermute | solution.py:24
  84.4 5.4 %collective-permute-start.16 = (f32[2,16,16,3]{3,2,1,0:T(8,128)S(1)}, f32[2,16,16,3]{3,2,1,0:T(8,128)S(1)}, u32[]{:S(2)}, u32[]{:S(2)}) collective-permute-start(f32[2,16,16,3]{3,2,1,0:T(8,128)S(1)} %get-tuple-element.19), channel_id=1, source_target_pairs={{0,1},{2,3},{4,5},{6,7},{8,9},{10,11},{12,13},{14,15},{16,17},{18,... | collective-permute-start | bytes 18440 | tf_op jit(solution)/shard_map/ppermute | solution.py:22
  85.9 8.7 %collective-permute-start.17 = (f32[2,16,16,3]{3,2,1,0:T(8,128)S(1)}, f32[2,16,16,3]{3,2,1,0:T(8,128)S(1)}, u32[]{:S(2)}, u32[]{:S(2)}) collective-permute-start(f32[2,16,16,3]{3,2,1,0:T(8,128)S(1)} %get-tuple-element.20), channel_id=1, source_target_pairs={{1,0},{3,2},{5,4},{7,6},{9,8},{11,10},{13,12},{15,14},{17,16},{19,... | collective-permute-start | bytes 18440 | tf_op jit(solution)/shard_map/ppermute | solution.py:24
  99.0 6.6 %collective-permute-start.19 = (f32[2,3,10,130]{3,2,1,0:T(8,128)S(1)}, f32[2,3,10,130]{3,2,1,0:T(8,128)S(1)}, u32[]{:S(2)}, u32[]{:S(2)}) collective-permute-start(f32[2,3,10,130]{3,2,1,0:T(8,128)S(1)} %get-tuple-element.48), channel_id=1, source_target_pairs={{8,0},{16,8},{24,16},{9,1},{17,9},{25,17},{10,2},{18,10},{26,18},{... | collective-permute-start | bytes 93608 | tf_op jit(solution)/shard_map/ppermute | solution.py:24
  105.7 4.1 %collective-permute-start.20 = (f32[2,16,3,130]{3,2,1,0:T(4,128)S(1)}, f32[2,16,3,130]{3,2,1,0:T(4,128)S(1)}, u32[]{:S(2)}, u32[]{:S(2)}) collective-permute-start(f32[2,16,3,130]{3,2,1,0:T(4,128)S(1)} %get-tuple-element.17), channel_id=1, source_target_pairs={{0,2},{2,4},{4,6},{1,3},{3,5},{5,7},{8,10},{10,12},{12,14},{9,11},... | collective-permute-start | bytes 149768 | tf_op jit(solution)/shard_map/ppermute | solution.py:22
  108.4 4.9 %collective-permute-start.21 = (f32[2,16,3,130]{3,2,1,0:T(4,128)S(1)}, f32[2,16,3,130]{3,2,1,0:T(4,128)S(1)}, u32[]{:S(2)}, u32[]{:S(2)}) collective-permute-start(f32[2,16,3,130]{3,2,1,0:T(4,128)S(1)} %get-tuple-element.18), channel_id=1, source_target_pairs={{2,0},{4,2},{6,4},{3,1},{5,3},{7,5},{10,8},{12,10},{14,12},{11,9},... | collective-permute-start | bytes 149768 | tf_op jit(solution)/shard_map/ppermute | solution.py:24
  113.5 5.4 %collective-permute-start.22 = (f32[2,16,16,3]{3,2,1,0:T(8,128)S(1)}, f32[2,16,16,3]{3,2,1,0:T(8,128)S(1)}, u32[]{:S(2)}, u32[]{:S(2)}) collective-permute-start(f32[2,16,16,3]{3,2,1,0:T(8,128)S(1)} %get-tuple-element.15), channel_id=1, source_target_pairs={{0,1},{2,3},{4,5},{6,7},{8,9},{10,11},{12,13},{14,15},{16,17},{18,... | collective-permute-start | bytes 18440 | tf_op jit(solution)/shard_map/ppermute | solution.py:22
  115.0 8.7 %collective-permute-start.23 = (f32[2,16,16,3]{3,2,1,0:T(8,128)S(1)}, f32[2,16,16,3]{3,2,1,0:T(8,128)S(1)}, u32[]{:S(2)}, u32[]{:S(2)}) collective-permute-start(f32[2,16,16,3]{3,2,1,0:T(8,128)S(1)} %get-tuple-element.16), channel_id=1, source_target_pairs={{1,0},{3,2},{5,4},{7,6},{9,8},{11,10},{13,12},{15,14},{17,16},{19,... | collective-permute-start | bytes 18440 | tf_op jit(solution)/shard_map/ppermute | solution.py:24
  128.2 6.6 %collective-permute-start.25 = (f32[2,3,10,130]{3,2,1,0:T(8,128)S(1)}, f32[2,3,10,130]{3,2,1,0:T(8,128)S(1)}, u32[]{:S(2)}, u32[]{:S(2)}) collective-permute-start(f32[2,3,10,130]{3,2,1,0:T(8,128)S(1)} %get-tuple-element.46), channel_id=1, source_target_pairs={{8,0},{16,8},{24,16},{9,1},{17,9},{25,17},{10,2},{18,10},{26,18},{... | collective-permute-start | bytes 93608 | tf_op jit(solution)/shard_map/ppermute | solution.py:24
  137.6 4.9 %collective-permute-start.27 = (f32[2,16,3,130]{3,2,1,0:T(4,128)S(1)}, f32[2,16,3,130]{3,2,1,0:T(4,128)S(1)}, u32[]{:S(2)}, u32[]{:S(2)}) collective-permute-start(f32[2,16,3,130]{3,2,1,0:T(4,128)S(1)} %get-tuple-element.14), channel_id=1, source_target_pairs={{2,0},{4,2},{6,4},{3,1},{5,3},{7,5},{10,8},{12,10},{14,12},{11,9},... | collective-permute-start | bytes 149768 | tf_op jit(solution)/shard_map/ppermute | solution.py:24
  142.7 5.4 %collective-permute-start.28 = (f32[2,16,16,3]{3,2,1,0:T(8,128)S(1)}, f32[2,16,16,3]{3,2,1,0:T(8,128)S(1)}, u32[]{:S(2)}, u32[]{:S(2)}) collective-permute-start(f32[2,16,16,3]{3,2,1,0:T(8,128)S(1)} %get-tuple-element.11), channel_id=1, source_target_pairs={{0,1},{2,3},{4,5},{6,7},{8,9},{10,11},{12,13},{14,15},{16,17},{18,... | collective-permute-start | bytes 18440 | tf_op jit(solution)/shard_map/ppermute | solution.py:22
  144.2 8.7 %collective-permute-start.29 = (f32[2,16,16,3]{3,2,1,0:T(8,128)S(1)}, f32[2,16,16,3]{3,2,1,0:T(8,128)S(1)}, u32[]{:S(2)}, u32[]{:S(2)}) collective-permute-start(f32[2,16,16,3]{3,2,1,0:T(8,128)S(1)} %get-tuple-element.12), channel_id=1, source_target_pairs={{1,0},{3,2},{5,4},{7,6},{9,8},{11,10},{13,12},{15,14},{17,16},{19,... | collective-permute-start | bytes 18440 | tf_op jit(solution)/shard_map/ppermute | solution.py:24
  (9 other events, 25.0 us)
where the time goes:
time: 199 us; the launch traced here: 198 us
  waiting for transfers between devices  80.1 us (40%)
  starting transfers between devices  56.7 us (28%)
  blocking collectives  38.8 us (19%)
  other arithmetic  13.6 us (7%)
  local copies, waits for them, and re-layouts  5.35 us (3%)
    ppermute x15, waiting for transfers between devices, extended(): lax.ppermute(head, axis, [((i + 1) % count, i) for i in range(ends)])  63.1 us
    psum x1, blocking collectives, local(): lax.psum((inner_table(basis_rows, image_rows), inner_vector(basis_rows, t...  38.8 us
    ppermute x15, starting transfers between devices, extended(): lax.ppermute(tail, axis, [(i, (i + 1) % count) for i in range(ends)])  37.1 us
    ppermute x15, starting transfers between devices, extended(): lax.ppermute(head, axis, [((i + 1) % count, i) for i in range(ends)])  19.6 us
    ppermute x15, waiting for transfers between devices, extended(): lax.ppermute(tail, axis, [(i, (i + 1) % count) for i in range(ends)])  17 us
  transfers between devices with their start and end apart: 30, of which 25 were waited for; matrix products, arithmetic and copies ran while one was open for 0% of the time, Pallas kernels for 0%

commit v1 on v0

v1 whole, which is shorter than its diff:
```python
import functools

import jax
import jax.numpy as jnp
from jax import lax
from jax.experimental import pallas as pl
from jax.experimental.pallas import tpu as pltpu
from jax.sharding import PartitionSpec as P

STEPS = 4
SWEEPS = 3
LANES = 128
MESH = pl.DeviceIdType.MESH
HIGHEST = lax.Precision.HIGHEST


def shift_lanes(values, amount):
    amount = amount % LANES
    return values if amount == 0 else pltpu.roll(values, amount, 1)


def kernel(
    counts, dims, res_ref, dir_ref, pow_ref, gram_ref, proj_ref,
    v_ref, t_ref, ysend, yrecv, zsend, zrecv, xsend, xrecv,
    red0, red1, red2,
    ys_sem, yr_sem, zs_sem, zr_sem, xs_sem, xr_sem,
    s0_sem, r0_sem, s1_sem, r1_sem, s2_sem, r2_sem,
):
    nx, ny, nz = counts
    cx, cy, cz = dims
    pitch = cy + 4
    rows = cz + 16
    gx, gy, gz = lax.axis_index("gx"), lax.axis_index("gy"), lax.axis_index("gz")
    here = {"gx": gx, "gy": gy, "gz": gz}
    size = {"gx": nx, "gy": ny, "gz": nz}

    def exists(offset):
        ok = None
        for axis, step in offset.items():
            if step == 0:
                continue
            test = here[axis] + step >= 0 if step < 0 else here[axis] + step < size[axis]
            ok = test if ok is None else jnp.logical_and(ok, test)
        return ok

    def target(offset):
        return {axis: here[axis] + step for axis, step in offset.items() if step != 0}

    yz_offsets = [{"gy": dy, "gz": dz} for dy in (-1, 0, 1) for dz in (-1, 1)]
    y_offsets = [{"gy": -1}, {"gy": 1}]
    x_offsets = [{"gx": -1}, {"gx": 1}]
    diagonals = [o for o in yz_offsets if o["gy"] != 0]

    barrier = pltpu.get_barrier_semaphore()
    expected = (nx - 1) + (ny - 1) + (nz - 1)
    for axis in ("gx", "gy", "gz"):
        for k in range(1, size[axis]):
            other = lax.rem(here[axis] + k, size[axis])
            pl.semaphore_signal(barrier, inc=1, device_id={axis: other}, device_id_type=MESH)
    for offset in diagonals:
        there = exists(offset)
        expected = expected + there.astype(jnp.int32)

        @pl.when(there)
        def _():
            pl.semaphore_signal(barrier, inc=1, device_id=target(offset), device_id_type=MESH)

    lane = lax.broadcasted_iota(jnp.int32, (rows, LANES), 1)
    row = lax.broadcasted_iota(jnp.int32, (rows, LANES), 0)
    slot_x = lane // pitch
    slot_y = lane - slot_x * pitch
    at_x, at_y, at_z = slot_x - 1, slot_y - 2, row - 8
    own = (at_x >= 0) & (at_x < cx) & (at_y >= 0) & (at_y < cy) & (at_z >= 0) & (at_z < cz)
    sub = (
        (at_x >= -1) & (at_x <= cx) & (at_y >= -1) & (at_y <= cy) & (at_z >= -1) & (at_z <= cz)
        & (gx * cx + at_x >= 0) & (gx * cx + at_x < nx * cx)
        & (gy * cy + at_y >= 0) & (gy * cy + at_y < ny * cy)
        & (gz * cz + at_z >= 0) & (gz * cz + at_z < nz * cz)
    )

    pick_cell = lax.broadcasted_iota(jnp.int32, (cx * cy, LANES), 0)
    pick_lane = lax.broadcasted_iota(jnp.int32, (cx * cy, LANES), 1)
    pick = (pick_lane == (pick_cell // cy + 1) * pitch + pick_cell % cy + 2).astype(jnp.float32)

    def spread(block_ref):
        flat = block_ref[...].reshape(cx * cy, cz)
        return lax.dot_general(
            flat, pick, (((0,), (0,)), ((), ())), precision=HIGHEST,
            preferred_element_type=jnp.float32,
        )

    def collect(field):
        flat = lax.dot_general(
            pick, field, (((1,), (1,)), ((), ())), precision=HIGHEST,
            preferred_element_type=jnp.float32,
        )
        return flat.reshape(cx, cy, cz)

    def neighbours(u):
        return (
            jnp.where(lane >= pitch, shift_lanes(u, pitch), 0.0)
            + jnp.where(lane < cx * pitch + pitch, shift_lanes(u, -pitch), 0.0) + shift_lanes(u, 1) + shift_lanes(u, -1)
            + pltpu.roll(u, 1, 0) + pltpu.roll(u, rows - 1, 0)
        )

    edge = jnp.zeros((8, LANES), jnp.float32)
    residual_rows = spread(res_ref)
    u0 = jnp.concatenate([edge, spread(dir_ref), edge], axis=0)
    u1 = jnp.concatenate([edge, residual_rows, edge], axis=0)
    v_ref[2 * STEPS + 1] = residual_rows
    t_ref[...] = jnp.zeros_like(t_ref)
    for index, offset in enumerate(y_offsets):
        @pl.when(jnp.logical_not(exists({"gy": -offset["gy"]})))
        def _():
            for r in range(STEPS + 1):
                yrecv[r, index] = jnp.zeros((rows, LANES), jnp.float32)
    for index, offset in enumerate(x_offsets):
        @pl.when(jnp.logical_not(exists({"gx": -offset["gx"]})))
        def _():
            for r in range(STEPS + 1):
                xrecv[r, index] = jnp.zeros((rows, LANES), jnp.float32)
    for index, offset in enumerate(yz_offsets):
        @pl.when(jnp.logical_not(exists({k: -s for k, s in offset.items()})))
        def _():
            for r in range(STEPS + 1):
                zrecv[r, index] = jnp.zeros((8, LANES), jnp.float32)

    pl.semaphore_wait(barrier, expected)

    def copy_y(r, index):
        return pltpu.make_async_remote_copy(
            ysend.at[r, index], yrecv.at[r, index], ys_sem.at[r, index], yr_sem.at[r, index],
            device_id=target(y_offsets[index]), device_id_type=MESH)

    def copy_x(r, index):
        return pltpu.make_async_remote_copy(
            xsend.at[r, index], xrecv.at[r, index], xs_sem.at[r, index], xr_sem.at[r, index],
            device_id=target(x_offsets[index]), device_id_type=MESH)

    def copy_z(r, index):
        side = 0 if yz_offsets[index]["gz"] < 0 else 1
        return pltpu.make_async_remote_copy(
            zsend.at[r, side], zrecv.at[r, index], zs_sem.at[r, index], zr_sem.at[r, index],
            device_id=target(yz_offsets[index]), device_id_type=MESH)

    def start(make, r, offsets):
        for index, offset in enumerate(offsets):
            @pl.when(exists(offset))
            def _():
                make(r, index).start()

    def wait(make, r, offsets):
        for index, offset in enumerate(offsets):
            @pl.when(exists({k: -s for k, s in offset.items()}))
            def _():
                make(r, index).wait_recv()

    def wait_sent(make, r, offsets):
        for index, offset in enumerate(offsets):
            @pl.when(exists(offset))
            def _():
                make(r, index).wait_send()

    def dot_rows(a, b):
        return jnp.sum(a * b, axis=0, keepdims=True)

    total = 2 * STEPS + 1
    pending = None

    def account(r, images):
        fresh = [r] + ([STEPS + r] if r > 0 else [])
        done = list(range(r + 1)) + [STEPS + 1 + k for k in range(r)]
        for a in fresh:
            image = images[0] if a == r else images[1]
            for b in done:
                if a == r and b == STEPS + r and r > 0:
                    continue
                part = dot_rows(v_ref[b], image)
                t_ref[pl.ds(a * total + b, 1), :] = part
                if a != b:
                    t_ref[pl.ds(b * total + a, 1), :] = part
            t_ref[pl.ds(total * total + a, 1), :] = dot_rows(v_ref[a], v_ref[total])

    def emit(r):
        if r > 0:
            pow_ref[0, r - 1] = collect(v_ref[r])
            pow_ref[1, r - 1] = collect(v_ref[STEPS + r])

    low = lambda v: jnp.where(slot_y < 3, v, 0.0)
    span = lambda start_lane, stop_lane: (lane >= start_lane) & (lane < stop_lane)
    top = cx * pitch
    for r in range(STEPS + 1):
        for side, head in ((0, 7), (1, cz + 6)):
            zsend[r, side] = jnp.concatenate(
                [u0[head:head + 3], u1[head:head + 3], jnp.zeros((2, LANES), jnp.float32)], axis=0)
        ysend[r, 0] = jnp.where(slot_y >= 9, shift_lanes(u0, cy), shift_lanes(u1, cy - 3))
        ysend[r, 1] = jnp.where(slot_y < 3, shift_lanes(u0, -cy), shift_lanes(u1, 3 - cy))
        start(copy_z, r, yz_offsets)
        start(copy_y, r, y_offsets)
        if pending is not None:
            account(r - 1, pending)
            emit(r - 1)
        wait(copy_y, r, y_offsets)
        from_above, from_below = yrecv[r, 0], yrecv[r, 1]
        p0 = u0 + jnp.where(slot_y >= 9, from_above, 0.0) + low(from_below)
        p1 = (
            u1 + jnp.where(slot_y >= 9, shift_lanes(from_above, 3), 0.0)
            + low(shift_lanes(from_below, -3))
        )
        wait(copy_z, r, yz_offsets)
        tile_slot = slot_y[:8]
        tiles = []
        for side in (0, 1):
            mid = zrecv[r, 2 + side]
            down = jnp.where(tile_slot >= 9, shift_lanes(zrecv[r, side], cy), 0.0)
            up = jnp.where(tile_slot < 3, shift_lanes(zrecv[r, 4 + side], -cy), 0.0)
            tiles.append(mid + down + up)

        def with_tiles(p, first):
            upper, lower = tiles[0][first:first + 3], tiles[1][first:first + 3]
            zero = lambda n: jnp.zeros((n, LANES), jnp.float32)
            head = p[:16] + jnp.concatenate([zero(6), lower, zero(7)], axis=0)
            tail = p[rows - 16:] + jnp.concatenate([zero(7), upper, zero(6)], axis=0)
            return jnp.concatenate([head, p[16:rows - 16], tail], axis=0)

        p0, p1 = with_tiles(p0, 0), with_tiles(p1, 3)
        width = 3 * pitch
        xsend[r, 0] = jnp.where(lane < width, p0, shift_lanes(p1, width))
        far = (cx - 1) * pitch
        xsend[r, 1] = jnp.where(lane < width, shift_lanes(p0, -far), shift_lanes(p1, width - far))
        start(copy_x, r, x_offsets)
        wait(copy_x, r, x_offsets)
        beyond, before = xrecv[r, 0], xrecv[r, 1]
        at_low, at_high = span(0, 2 * pitch), span(top, top + 2 * pitch)
        ext_low, ext_high = span(0, pitch), span(top + pitch, top + 2 * pitch)

        def with_x(p, first):
            main = (
                p + jnp.where(at_low, shift_lanes(before, -first - pitch), 0.0)
                + jnp.where(at_high, shift_lanes(beyond, top - first), 0.0)
            )
            far_cells = (
                jnp.where(ext_low, shift_lanes(before, -first), 0.0)
                + jnp.where(ext_high, shift_lanes(beyond, top - pitch - first), 0.0)
            )
            return main, far_cells

        p0, far0 = with_x(p0, 0)
        p1, far1 = with_x(p1, width)
        p0 = jnp.where(lane < top + 2 * pitch, p0, 0.0)
        p1 = jnp.where(lane < top + 2 * pitch, p1, 0.0)
        b0 = jnp.where(sub, 6.0 * p0 - neighbours(p0) - far0, 0.0)
        a1 = jnp.where(sub, 6.0 * p1 - neighbours(p1) - far1, 0.0)
        b1 = jnp.where(sub, p1, 0.0) if r == 0 else a1
        v_ref[r] = jnp.where(own, p0, 0.0)[8:8 + cz]
        if r > 0:
            v_ref[STEPS + r] = jnp.where(own, p1, 0.0)[8:8 + cz]
        pending = (b0[8:8 + cz], a1[8:8 + cz])
        if r < STEPS:
            c0, c1 = b0 * (1.0 / 9.0), b1 * (1.0 / 9.0)
            u0, u1 = c0, c1
            for _ in range(SWEEPS - 1):
                u0 = jnp.where(sub, c0 + u0 * (1.0 / 3.0) + neighbours(u0) * (1.0 / 9.0), 0.0)
                u1 = jnp.where(sub, c1 + u1 * (1.0 / 3.0) + neighbours(u1) * (1.0 / 9.0), 0.0)

    account(STEPS, pending)
    value = lax.dot_general(
        jnp.ones((8, LANES), jnp.float32), t_ref[...], (((1,), (1,)), ((), ())),
        precision=HIGHEST, preferred_element_type=jnp.float32)

    def gather(value, axis, buffer, s_sem, r_sem, first):
        me, n = here[axis], size[axis]
        buffer[0] = value
        def make(k):
            return pltpu.make_async_remote_copy(
                buffer.at[0], buffer.at[k], s_sem.at[k], r_sem.at[k],
                device_id={axis: lax.rem(me + k, n)}, device_id_type=MESH)
        for k in range(1, n):
            make(k).start()
        if first:
            emit(STEPS)
        for k in range(1, n):
            make(k).wait_recv()
        result = jnp.zeros_like(value)
        for g in range(n):
            result = result + buffer[lax.rem(me + n - g, n)]
        for k in range(1, n):
            make(k).wait_send()
        return result

    value = gather(value, "gy", red0, s0_sem, r0_sem, True)
    value = gather(value, "gx", red1, s1_sem, r1_sem, False)
    value = gather(value, "gz", red2, s2_sem, r2_sem, False)
    value = value * (1.0 / (nx * cx * ny * cy * nz * cz))
    for a in range(total):
        gram_ref[a:a + 1, :] = value[0:1, a * total:(a + 1) * total]
    proj_ref[...] = value[0:1, total * total:total * total + total]
    for r in range(STEPS + 1):
        wait_sent(copy_y, r, y_offsets)
        wait_sent(copy_z, r, yz_offsets)
        wait_sent(copy_x, r, x_offsets)


def solution(mesh):
    counts = tuple(mesh.shape[a] for a in ("gx", "gy", "gz"))

    def local(residual, direction):
        dims = residual.shape
        rows = dims[2] + 16
        total = 2 * STEPS + 1
        rounds = STEPS + 1
        f32 = jnp.float32
        dma = pltpu.SemaphoreType.DMA
        vm = pl.BlockSpec(memory_space=pltpu.VMEM)
        powers, gram, proj = pl.pallas_call(
            functools.partial(kernel, counts, dims),
            out_shape=(
                jax.ShapeDtypeStruct((2, STEPS) + dims, f32),
                jax.ShapeDtypeStruct((total, total), f32),
                jax.ShapeDtypeStruct((1, total), f32),
            ),
            in_specs=[vm, vm],
            out_specs=(vm, vm, vm),
            scratch_shapes=[
                pltpu.VMEM((total + 1, dims[2], LANES), f32),
                pltpu.VMEM((LANES, LANES), f32),
                pltpu.VMEM((rounds, 2, rows, LANES), f32),
                pltpu.VMEM((rounds, 2, rows, LANES), f32),
                pltpu.VMEM((rounds, 2, 8, LANES), f32),
                pltpu.VMEM((rounds, 6, 8, LANES), f32),
                pltpu.VMEM((rounds, 2, rows, LANES), f32),
                pltpu.VMEM((rounds, 2, rows, LANES), f32),
                pltpu.VMEM((counts[1], 8, LANES), f32),
                pltpu.VMEM((counts[0], 8, LANES), f32),
                pltpu.VMEM((counts[2], 8, LANES), f32),
                dma((rounds, 2)), dma((rounds, 2)),
                dma((rounds, 6)), dma((rounds, 6)),
                dma((rounds, 2)), dma((rounds, 2)),
                dma((counts[1],)), dma((counts[1],)),
                dma((counts[0],)), dma((counts[0],)),
                dma((counts[2],)), dma((counts[2],)),
            ],
            compiler_params=pltpu.CompilerParams(collective_id=0, has_side_effects=True),
            name="powers_basis",
        )(residual, direction)
        return powers, gram, proj.reshape(total)

    placed = (P("gx", "gy", "gz"), P("gx", "gy", "gz"))
    return jax.shard_map(
        local,
        mesh=mesh,
        in_specs=placed,
        out_specs=(P(None, None, "gx", "gy", "gz"), P(), P()),
        check_vma=False,
    )
```

time: 199 us -> 58 us (0.29)
  waiting for transfers between devices: 80.1 us -> 0 us
  starting transfers between devices: 56.7 us -> 0 us
  Pallas kernels: 0 us -> 54.3 us
  blocking collectives: 38.8 us -> 0 us
  other arithmetic: 13.6 us -> 0 us
  local copies, waits for them, and re-layouts: 5.35 us -> 2.87 us
    ppermute x30 -> x0, waiting for transfers between devices: 80.1 us -> none  [the longest x15 63.1 us: extended(): lax.ppermute(head, axis, [((i + 1) % count, i) for i in range(ends)])]
    ppermute x30 -> x0, starting transfers between devices: 56.7 us -> none  [the longest x15 37.1 us: extended(): lax.ppermute(tail, axis, [(i, (i + 1) % count) for i in range(ends)])]
    pallas_call x0 -> x1, Pallas kernels: none -> 54.3 us  [local(): pl.pallas_call(functools.partial(kernel, counts, dims), out_shape=(jax.Sh...]
    psum x1 -> x0, blocking collectives: 38.8 us -> none  [local(): lax.psum((inner_table(basis_rows, image_rows), inner_vector(basis_rows, t...]
    mul x14 -> x0, other arithmetic: 4.48 us -> none  [the longest x8 2.53 us: subdomain_solve(): iterate = mask * (iterate + SWEEP_SCALE * (source - stencil_image(padded)))]
    slice x47 -> x0, local copies, waits for them, and re-layouts: 3.36 us -> none  [the longest x15 1.09 us: assemble(): middle = lax.slice_in_dim(received, reach, reach + length, axis=dimension)]
    concatenate x10 -> x0, other arithmetic: 2.72 us -> none  [extended(): jnp.concatenate([lax.ppermute(tail, axis, [(i, (i + 1) % count) for i in...]
    add x15 -> x0, other arithmetic: 2.57 us -> none  [assemble(): middle + pad_along(below_part, dimension, 0, result_len - reach)]
  transfers between devices with their start and end apart: 30 -> 0, of which waited for: 25 -> 0; matrix products, arithmetic and copies ran while one was open for 0% -> 0% of each run, Pallas kernels for 0% -> 0%
where the time goes in v1:
time: 58 us; the launch traced here: 57.8 us
  Pallas kernels  54.3 us (94%)
  local copies, waits for them, and re-layouts  2.87 us (5%)
  between operations  0.65 us (1%)
    pallas_call x1, Pallas kernels, local(): pl.pallas_call(functools.partial(kernel, counts, dims), out_shape=(jax.Sh...  54.3 us
    unnamed x7, local copies, waits for them, and re-layouts  2.87 us

profile of v1, /device:TPU:0, one launch (start us, length us, event | category | flops | bytes accessed | tf_op | source)
XLA Modules:
  0.0 57.8 jit_solution(15240275169159706354)
XLA Ops:
  0.6 54.3 %powers_basis.1 = (f32[2,4,8,8,128]{4,3,2,1,0:T(8,128)}, f32[9,9]{1,0:T(8,128)}, f32[1,9]{1,0:T(1,128)}) custom-call(f32[8,8,128]{2,1,0:T(8,128)} %res_ref.1, f32[8,8,128]{2,1,0:T(8,128)} %dir_ref.1), custom_call_target="tpu_custom_call" | custom-call | tf_op jit(solution)/shard_map/powers_basis/pallas_call | solution.py:315
  54.9 0.0 copy-start
  54.9 1.7 %copy.8 = f32[2,4,8,8,128]{4,3,2,1,0:T(8,128)} copy(f32[2,4,8,8,128]{4,3,2,1,0:T(8,128)} %get-tuple-element.12) | data formatting | bytes 524288
  56.6 0.0 copy-done
  56.6 0.0 copy-start.1
  56.6 0.6 %copy.9 = f32[9,9]{1,0:T(8,128)} copy(f32[9,9]{1,0:T(8,128)S(1)} %copy-done) | data formatting | bytes 648
  57.2 0.1 copy-done.1
  57.3 0.5 copy.10
Async XLA Ops:
  54.9 1.7 %copy-start = (f32[9,9]{1,0:T(8,128)S(1)}, f32[9,9]{1,0:T(8,128)}, u32[]{:S(2)}) copy-start(f32[9,9]{1,0:T(8,128)} %get-tuple-element.13) | copy-start | bytes 976
  56.6 0.7 %copy-start.1 = (f32[1,9]{1,0:T(1,128)S(1)}, f32[1,9]{1,0:T(1,128)}, u32[]{:S(2)}) copy-start(f32[1,9]{1,0:T(1,128)} %get-tuple-element.8) | copy-start | bytes 112

commit v2 on v1

--- a/solution.py
+++ b/solution.py
@@ -22,9 +22,9 @@
 def kernel(
     counts, dims, res_ref, dir_ref, pow_ref, gram_ref, proj_ref,
     v_ref, t_ref, ysend, yrecv, zsend, zrecv, xsend, xrecv,
-    red0, red1, red2,
+    red0, red1,
     ys_sem, yr_sem, zs_sem, zr_sem, xs_sem, xr_sem,
-    s0_sem, r0_sem, s1_sem, r1_sem, s2_sem, r2_sem,
+    s0_sem, r0_sem, s1_sem, r1_sem,
 ):
     nx, ny, nz = counts
     cx, cy, cz = dims
@@ -49,21 +49,25 @@
     yz_offsets = [{"gy": dy, "gz": dz} for dy in (-1, 0, 1) for dz in (-1, 1)]
     y_offsets = [{"gy": -1}, {"gy": 1}]
     x_offsets = [{"gx": -1}, {"gx": 1}]
-    diagonals = [o for o in yz_offsets if o["gy"] != 0]
 
     barrier = pltpu.get_barrier_semaphore()
-    expected = (nx - 1) + (ny - 1) + (nz - 1)
-    for axis in ("gx", "gy", "gz"):
-        for k in range(1, size[axis]):
-            other = lax.rem(here[axis] + k, size[axis])
-            pl.semaphore_signal(barrier, inc=1, device_id={axis: other}, device_id_type=MESH)
-    for offset in diagonals:
-        there = exists(offset)
-        expected = expected + there.astype(jnp.int32)
-
-        @pl.when(there)
-        def _():
-            pl.semaphore_signal(barrier, inc=1, device_id=target(offset), device_id_type=MESH)
+    expected = (nx - 1) + (ny * nz - 1)
+
+    def in_line(k):
+        return {"gx": lax.rem(gx + k, nx)}
+
+    def in_plane(k):
+        ky, kz = divmod(k, nz)
+        place = {}
+        if ky:
+            place["gy"] = lax.rem(gy + ky, ny)
+        if kz:
+            place["gz"] = lax.rem(gz + kz, nz)
+        return place
+
+    for count, place in ((nx, in_line), (ny * nz, in_plane)):
+        for k in range(1, count):
+            pl.semaphore_signal(barrier, inc=1, device_id=place(k), device_id_type=MESH)
 
     lane = lax.broadcasted_iota(jnp.int32, (rows, LANES), 1)
     row = lax.broadcasted_iota(jnp.int32, (rows, LANES), 0)
@@ -199,7 +203,6 @@
         start(copy_y, r, y_offsets)
         if pending is not None:
             account(r - 1, pending)
-            emit(r - 1)
         wait(copy_y, r, y_offsets)
         from_above, from_below = yrecv[r, 0], yrecv[r, 1]
         p0 = u0 + jnp.where(slot_y >= 9, from_above, 0.0) + low(from_below)
@@ -229,6 +232,8 @@
         far = (cx - 1) * pitch
         xsend[r, 1] = jnp.where(lane < width, shift_lanes(p0, -far), shift_lanes(p1, width - far))
         start(copy_x, r, x_offsets)
+        if r > 0:
+            emit(r - 1)
         wait(copy_x, r, x_offsets)
         beyond, before = xrecv[r, 0], xrecv[r, 1]
         at_low, at_high = span(0, 2 * pitch), span(top, top + 2 * pitch)
@@ -268,29 +273,34 @@
         jnp.ones((8, LANES), jnp.float32), t_ref[...], (((1,), (1,)), ((), ())),
         precision=HIGHEST, preferred_element_type=jnp.float32)
 
-    def gather(value, axis, buffer, s_sem, r_sem, first):
-        me, n = here[axis], size[axis]
+    def gather(value, count, place, slots, buffer, s_sem, r_sem, first):
         buffer[0] = value
+
         def make(k):
             return pltpu.make_async_remote_copy(
                 buffer.at[0], buffer.at[k], s_sem.at[k], r_sem.at[k],
-                device_id={axis: lax.rem(me + k, n)}, device_id_type=MESH)
-        for k in range(1, n):
+                device_id=place(k), device_id_type=MESH)
+
+        for k in range(1, count):
             make(k).start()
         if first:
             emit(STEPS)
-        for k in range(1, n):
+        for k in range(1, count):
             make(k).wait_recv()
         result = jnp.zeros_like(value)
-        for g in range(n):
-            result = result + buffer[lax.rem(me + n - g, n)]
-        for k in range(1, n):
+        for slot in slots:
+            result = result + buffer[slot]
+        for k in range(1, count):
             make(k).wait_send()
         return result
 
-    value = gather(value, "gy", red0, s0_sem, r0_sem, True)
-    value = gather(value, "gx", red1, s1_sem, r1_sem, False)
-    value = gather(value, "gz", red2, s2_sem, r2_sem, False)
+    plane_slots = [
+        lax.rem(gy + ny - g, ny) * nz + lax.rem(gz + nz - h, nz)
+        for g in range(ny) for h in range(nz)
+    ]
+    line_slots = [lax.rem(gx + nx - g, nx) for g in range(nx)]
+    value = gather(value, ny * nz, in_plane, plane_slots, red0, s0_sem, r0_sem, True)
+    value = gather(value, nx, in_line, line_slots, red1, s1_sem, r1_sem, False)
     value = value * (1.0 / (nx * cx * ny * cy * nz * cz))
     for a in range(total):
         gram_ref[a:a + 1, :] = value[0:1, a * total:(a + 1) * total]
@@ -330,15 +340,13 @@
                 pltpu.VMEM((rounds, 6, 8, LANES), f32),
                 pltpu.VMEM((rounds, 2, rows, LANES), f32),
                 pltpu.VMEM((rounds, 2, rows, LANES), f32),
-                pltpu.VMEM((counts[1], 8, LANES), f32),
+                pltpu.VMEM((counts[1] * counts[2], 8, LANES), f32),
                 pltpu.VMEM((counts[0], 8, LANES), f32),
-                pltpu.VMEM((counts[2], 8, LANES), f32),
                 dma((rounds, 2)), dma((rounds, 2)),
                 dma((rounds, 6)), dma((rounds, 6)),
                 dma((rounds, 2)), dma((rounds, 2)),
-                dma((counts[1],)), dma((counts[1],)),
+                dma((counts[1] * counts[2],)), dma((counts[1] * counts[2],)),
                 dma((counts[0],)), dma((counts[0],)),
-                dma((counts[2],)), dma((counts[2],)),
             ],
             compiler_params=pltpu.CompilerParams(collective_id=0, has_side_effects=True),
             name="powers_basis",

time: 58 us -> 55.6 us (0.959)
  Pallas kernels: 54.3 us -> 51.9 us
    pallas_call x1, Pallas kernels: 54.3 us -> 51.9 us  [local(): pl.pallas_call(functools.partial(kernel, counts, dims), out_shape=(jax.Sh...]
where the time goes in v2:
time: 55.6 us; the launch traced here: 55.4 us
  Pallas kernels  51.9 us (93%)
  local copies, waits for them, and re-layouts  2.87 us (5%)
  between operations  0.65 us (1%)
    pallas_call x1, Pallas kernels, local(): pl.pallas_call(functools.partial(kernel, counts, dims), out_shape=(jax.Sh...  51.9 us
    unnamed x7, local copies, waits for them, and re-layouts  2.87 us

profile of v2, /device:TPU:0, one launch (start us, length us, event | category | flops | bytes accessed | tf_op | source)
XLA Modules:
  0.0 55.4 jit_solution(1383204819106254284)
XLA Ops:
  0.6 51.9 %powers_basis.1 = (f32[2,4,8,8,128]{4,3,2,1,0:T(8,128)}, f32[9,9]{1,0:T(8,128)}, f32[1,9]{1,0:T(1,128)}) custom-call(f32[8,8,128]{2,1,0:T(8,128)} %res_ref.1, f32[8,8,128]{2,1,0:T(8,128)} %dir_ref.1), custom_call_target="tpu_custom_call" | custom-call | tf_op jit(solution)/shard_map/powers_basis/pallas_call | solution.py:325
  52.5 0.0 copy-start
  52.5 1.7 %copy.8 = f32[2,4,8,8,128]{4,3,2,1,0:T(8,128)} copy(f32[2,4,8,8,128]{4,3,2,1,0:T(8,128)} %get-tuple-element.12) | data formatting | bytes 524288
  54.2 0.0 copy-done
  54.2 0.0 copy-start.1
  54.2 0.6 %copy.9 = f32[9,9]{1,0:T(8,128)} copy(f32[9,9]{1,0:T(8,128)S(1)} %copy-done) | data formatting | bytes 648
  54.8 0.1 copy-done.1
  54.9 0.5 copy.10
Async XLA Ops:
  52.5 1.7 %copy-start = (f32[9,9]{1,0:T(8,128)S(1)}, f32[9,9]{1,0:T(8,128)}, u32[]{:S(2)}) copy-start(f32[9,9]{1,0:T(8,128)} %get-tuple-element.13) | copy-start | bytes 976
  54.2 0.7 %copy-start.1 = (f32[1,9]{1,0:T(1,128)S(1)}, f32[1,9]{1,0:T(1,128)}, u32[]{:S(2)}) copy-start(f32[1,9]{1,0:T(1,128)} %get-tuple-element.8) | copy-start | bytes 112

commit v3 on v2

--- a/solution.py
+++ b/solution.py
@@ -69,7 +69,7 @@
         for k in range(1, count):
             pl.semaphore_signal(barrier, inc=1, device_id=place(k), device_id_type=MESH)
 
-    lane = lax.broadcasted_iota(jnp.int32, (rows, LANES), 1)
+    lane = lax.broadcasted_iota(jnp.int32, (1, LANES), 1)
     row = lax.broadcasted_iota(jnp.int32, (rows, LANES), 0)
     slot_x = lane // pitch
     slot_y = lane - slot_x * pitch
@@ -211,7 +211,7 @@
             + low(shift_lanes(from_below, -3))
         )
         wait(copy_z, r, yz_offsets)
-        tile_slot = slot_y[:8]
+        tile_slot = slot_y
         tiles = []
         for side in (0, 1):
             mid = zrecv[r, 2 + side]

time: 55.6 us -> 55.6 us (level)
  no operation moved by 1% of the time
where the time goes in v3:
time: 55.6 us; the launch traced here: 55.4 us
  Pallas kernels  51.9 us (93%)
  local copies, waits for them, and re-layouts  2.87 us (5%)
  between operations  0.65 us (1%)
    pallas_call x1, Pallas kernels, local(): pl.pallas_call(functools.partial(kernel, counts, dims), out_shape=(jax.Sh...  51.9 us
    unnamed x7, local copies, waits for them, and re-layouts  2.87 us

profile of v3, /device:TPU:0, one launch (start us, length us, event | category | flops | bytes accessed | tf_op | source)
XLA Modules:
  0.0 55.4 jit_solution(4340722405056033616)
XLA Ops:
  0.6 51.9 %powers_basis.1 = (f32[2,4,8,8,128]{4,3,2,1,0:T(8,128)}, f32[9,9]{1,0:T(8,128)}, f32[1,9]{1,0:T(1,128)}) custom-call(f32[8,8,128]{2,1,0:T(8,128)} %res_ref.1, f32[8,8,128]{2,1,0:T(8,128)} %dir_ref.1), custom_call_target="tpu_custom_call" | custom-call | tf_op jit(solution)/shard_map/powers_basis/pallas_call | solution.py:325
  52.5 0.0 copy-start
  52.6 1.7 %copy.8 = f32[2,4,8,8,128]{4,3,2,1,0:T(8,128)} copy(f32[2,4,8,8,128]{4,3,2,1,0:T(8,128)} %get-tuple-element.12) | data formatting | bytes 524288
  54.2 0.0 copy-done
  54.2 0.0 copy-start.1
  54.2 0.6 %copy.9 = f32[9,9]{1,0:T(8,128)} copy(f32[9,9]{1,0:T(8,128)S(1)} %copy-done) | data formatting | bytes 648
  54.8 0.1 copy-done.1
  54.9 0.5 copy.10
Async XLA Ops:
  52.5 1.7 %copy-start = (f32[9,9]{1,0:T(8,128)S(1)}, f32[9,9]{1,0:T(8,128)}, u32[]{:S(2)}) copy-start(f32[9,9]{1,0:T(8,128)} %get-tuple-element.13) | copy-start | bytes 976
  54.2 0.7 %copy-start.1 = (f32[1,9]{1,0:T(1,128)S(1)}, f32[1,9]{1,0:T(1,128)}, u32[]{:S(2)}) copy-start(f32[1,9]{1,0:T(1,128)} %get-tuple-element.8) | copy-start | bytes 112
